TPU v7x, 256 devices: a whole 4x4x8 slice. The times are simulated.
256 devices in a mesh: group: 4 (over x), dp: 16 (over z_lo, y, core), mp: 4 (over z_hi).
Axes of the slice: x: 4, y: 4, z: 8 (z_hi: 4, z_lo: 2; z = z_hi * 2 + z_lo), core: 2. Of those that a mesh axis runs over, the one named last changes fastest.
Arguments:
- block_input: bfloat16 [768, 8192], P(None, 'dp'), may hold values from -6 to 6
- parent_gate_up: bfloat16 [2, 8192, 14336], P(None, 'dp', ('group', 'mp')), may hold values from -0.0625 to 0.0625
- parent_down: bfloat16 [14336, 8192], P(('group', 'mp'), 'dp'), may hold values from -0.046875 to 0.046875
- variant_gate_up: bfloat16 [4, 2, 8192, 3584], P('group', None, 'dp', 'mp'), may hold values from -0.0625 to 0.0625
- variant_down: bfloat16 [4, 3584, 8192], P('group', 'mp', 'dp'), may hold values from -0.09375 to 0.09375
- widths: int32 [4], P('group'), may hold values from 896 to 3584, as said below
Outputs:
- grad_gate_up: float32 [4, 2, 8192, 3584], P('group', None, 'dp', 'mp')
- grad_down: float32 [4, 3584, 8192], P('group', 'mp', 'dp')
Inputs may be any that keep to these rules, and one draw needn't show every extreme that they name: Variant v uses its hidden units 0 to widths[v] - 1; one variant uses all 3584 of them and another exactly a quarter of 3584.
All inputs are finite; a program needn't handle non-finite values.
Results may differ from a plain program's by a relative error of at most 0.008.
Values may be sent and summed in bfloat16 or wider, within the bound.
No kernel may reach another device: no remote copies, remote signals or barrier semaphores. Data moves between devices by JAX's collectives and lax.ppermute only.
A program may use at most 64 MiB of HBM per device.

v0:
```python
import math
import jax
import jax.numpy as jnp
from jax import lax
from jax.sharding import PartitionSpec as P


def gated_values(pre_act, unit_mask):
    gate_value = pre_act[:, 0].astype(jnp.float32)
    up_value = pre_act[:, 1].astype(jnp.float32)
    sigmoid_gate = jax.nn.sigmoid(gate_value)
    return (gate_value * sigmoid_gate * up_value * unit_mask).astype(jnp.bfloat16)


def pre_gradient(pre_act, unit_mask, hidden_grad):
    gate_value = pre_act[:, 0].astype(jnp.float32)
    up_value = pre_act[:, 1].astype(jnp.float32)
    sigmoid_gate = jax.nn.sigmoid(gate_value)
    masked_grad = hidden_grad * unit_mask
    grad_gate = masked_grad * up_value * sigmoid_gate * (1.0 + gate_value * (1.0 - sigmoid_gate))
    grad_up = masked_grad * gate_value * sigmoid_gate
    return jnp.stack([grad_gate, grad_up], axis=1).astype(jnp.bfloat16)


def body(block_input, parent_gate_up, parent_down, variant_gate_up, variant_down, widths):
    local_gate_up = variant_gate_up[0]
    local_down = variant_down[0]
    local_units = local_down.shape[0]
    all_tokens = block_input.shape[0]
    first_unit = lax.axis_index("mp") * local_units
    unit_index = first_unit + jnp.arange(local_units, dtype=jnp.int32)
    unit_mask = (unit_index < widths[0]).astype(jnp.float32)
    parent_term = jnp.einsum(
        "td,kdf->tkf", block_input, parent_gate_up, preferred_element_type=jnp.float32
    )
    variant_term = jnp.einsum(
        "td,kdf->tkf", block_input, local_gate_up, preferred_element_type=jnp.float32
    )
    parent_rows, variant_rows = (
        lax.psum_scatter(parent_term, "dp", scatter_dimension=0, tiled=True),
        lax.psum_scatter(variant_term, "dp", scatter_dimension=0, tiled=True),
    )
    parent_pre = parent_rows.astype(jnp.bfloat16)
    variant_pre = variant_rows.astype(jnp.bfloat16)
    parent_hidden = gated_values(parent_pre, 1.0)
    parent_all, variant_all = (
        lax.all_gather(parent_hidden, "dp", axis=0, tiled=True),
        lax.all_gather(variant_pre, "dp", axis=0, tiled=True),
    )
    variant_hidden = gated_values(variant_all, unit_mask)
    teacher_part = jnp.dot(parent_all, parent_down, preferred_element_type=jnp.float32)
    student_part = jnp.dot(variant_hidden, local_down, preferred_element_type=jnp.float32)
    teacher = lax.psum(teacher_part, ("group", "mp"))
    student = lax.psum(student_part, "mp")
    loss_scale = 1.0 / math.sqrt(all_tokens)
    output_grad = ((student - teacher) * loss_scale).astype(jnp.bfloat16)
    grad_down = lax.dot_general(
        variant_hidden, output_grad, (((0,), (0,)), ((), ())), preferred_element_type=jnp.float32
    )
    hidden_part = lax.dot_general(
        output_grad, local_down, (((1,), (1,)), ((), ())), preferred_element_type=jnp.float32
    )
    hidden_full = lax.psum(hidden_part, "dp")
    grad_pre = pre_gradient(variant_all, unit_mask, hidden_full)
    grad_gate_up = jnp.einsum(
        "td,tkf->kdf", block_input, grad_pre, preferred_element_type=jnp.float32
    )
    return (grad_gate_up[None], grad_down[None])


def solution(mesh):
    in_specs = (
        P(None, "dp"),
        P(None, "dp", ("group", "mp")),
        P(("group", "mp"), "dp"),
        P("group", None, "dp", "mp"),
        P("group", "mp", "dp"),
        P("group"),
    )
    out_specs = (P("group", None, "dp", "mp"), P("group", "mp", "dp"))
    return jax.shard_map(body, mesh=mesh, in_specs=in_specs, out_specs=out_specs, check_vma=False)
```

profile of v0, /device:TPU:1, one launch (start us, length us, event | category | flops | bytes accessed | tf_op | source)
XLA Modules:
  0.0 652.1 jit_solution(2625803845936884595)
XLA Ops:
  7.2 0.0 copy-start
  7.2 0.0 reduce-scatter.5.cloned.1.call-start
  7.2 1.4 copy-done
  8.7 5.2 fusion.45
  13.9 0.0 copy-start.1
  13.9 0.0 reduce-scatter.5.cloned.1.call-update
  13.9 0.0 reduce-scatter.3.cloned.1.call-start
  13.9 1.1 copy-done.1
  15.0 5.5 fusion.29
  20.5 0.0 reduce-scatter.3.cloned.1.call-update
  20.5 0.0 all-gather.5.cloned.1.call-start
  20.6 66.0 %reduce-scatter.5.cloned.1.call-done = f32[48,2,896]{2,0,1:T(8,128)} async-done(((f32[768,2,896]{2,0,1:T(8,128)}), f32[48,2,896]{2,0,1:T(8,128)}) %reduce-scatter.5.cloned.1.call-update) | async-done | bytes 344080 | tf_op jit(solution)/shard_map/reduce_scatter | solution.py:40
  86.6 1.0 convert_element_type.66
  87.6 0.7 fusion.52
  88.3 0.0 all-gather.5.cloned.1.call-update
  88.3 0.0 all-gather.3.cloned.1.call-start
  88.4 71.3 %reduce-scatter.3.cloned.1.call-done = f32[48,2,896]{2,0,1:T(8,128)} async-done(((f32[768,2,896]{2,0,1:T(8,128)}), f32[48,2,896]{2,0,1:T(8,128)}) %reduce-scatter.3.cloned.1.call-update) | async-done | bytes 344080 | tf_op jit(solution)/shard_map/reduce_scatter | solution.py:41
  159.7 1.7 convert_element_type.60
  161.3 0.0 all-gather.3.cloned.1.call-update
  161.3 0.0 copy-start.2
  161.4 0.0 all-reduce.6.cloned.1.call-start
  161.4 38.0 %all-gather.5.cloned.1.call-done = bf16[768,896]{1,0:T(8,128)(2,1)} async-done(((bf16[48,896]{1,0:T(8,128)(2,1)}), bf16[768,896]{1,0:T(8,128)(2,1)}) %all-gather.5.cloned.1.call-update) | async-done | bytes 1376272 | tf_op jit(solution)/shard_map/all_gather | solution.py:47
  199.4 3.7 fusion.57
  203.1 0.0 all-reduce.6.cloned.1.call-update
  203.1 0.0 all-reduce.4.cloned.1.call-start
  203.8 35.3 %all-gather.3.cloned.1.call-done = bf16[768,2,896]{2,0,1:T(8,128)(2,1)} async-done(((bf16[48,2,896]{2,0,1:T(8,128)(2,1)}), bf16[768,2,896]{2,0,1:T(8,128)(2,1)}) %all-gather.3.cloned.1.call-update) | async-done | bytes 2752528 | tf_op jit(solution)/shard_map/all_gather | solution.py:48
  239.1 0.0 copy-done.2
  239.1 4.0 fusion.31
  243.2 0.0 all-reduce.4.cloned.1.call-update
  243.2 0.0 all-reduce.8.cloned.1.call-start
  243.2 163.2 %all-reduce.6.cloned.1.call-done = f32[768,512]{1,0:T(8,128)} async-done(((f32[768,512]{1,0:T(8,128)}), f32[768,512]{1,0:T(8,128)}) %all-reduce.6.cloned.1.call-update) | async-done | bytes 1572880 | tf_op jit(solution)/shard_map/psum | solution.py:53
  406.4 93.0 %all-reduce.4.cloned.1.call-done = f32[768,512]{1,0:T(8,128)} async-done(((f32[768,512]{1,0:T(8,128)}), f32[768,512]{1,0:T(8,128)}) %all-reduce.4.cloned.1.call-update) | async-done | bytes 1572880 | tf_op jit(solution)/shard_map/psum | solution.py:54
  499.4 2.3 multiply_convert_fusion
  501.7 3.7 fusion.39
  505.4 0.0 all-reduce.8.cloned.1.call-update
  505.5 4.1 convolution_bitcast_fusion
  509.6 123.6 %all-reduce.8.cloned.1.call-done = f32[768,896]{1,0:T(8,128)} async-done(((f32[768,896]{1,0:T(8,128)}), f32[768,896]{1,0:T(8,128)}) %all-reduce.8.cloned.1.call-update) | async-done | bytes 2752528 | tf_op jit(solution)/shard_map/psum | solution.py:63
  633.2 4.0 fusion.36
  637.2 3.5 fusion.26
  640.7 4.6 copy.9
  (1 shorter events, 0.0 us)
Async XLA Ops:
  7.2 1.5 copy-start
  7.2 79.4 %reduce-scatter.5.cloned.1.call-start = ((), (), s32[]{:S(2)}) async-start(), calls=%async_computation.5 | async-start | bytes 5849088 | tf_op jit(solution)/shard_map/reduce_scatter | solution.py:40
  13.9 1.1 copy-start.1
  13.9 145.8 %reduce-scatter.3.cloned.1.call-start = ((), (), s32[]{:S(2)}) async-start(), calls=%async_computation.2 | async-start | bytes 5849088 | tf_op jit(solution)/shard_map/reduce_scatter | solution.py:41
  20.5 178.9 %all-gather.5.cloned.1.call-start = ((), (), s32[]{:S(2)}) async-start(), calls=%async_computation.6 | async-start | bytes 1462272 | tf_op jit(solution)/shard_map/all_gather | solution.py:47
  88.3 150.8 %all-gather.3.cloned.1.call-start = ((), (), s32[]{:S(2)}) async-start(), calls=%async_computation.3 | async-start | bytes 2924544 | tf_op jit(solution)/shard_map/all_gather | solution.py:48
  161.3 77.8 %copy-start.2 = (bf16[1,896,512]{2,1,0:T(8,128)(2,1)S(1)}, bf16[1,896,512]{2,1,0:T(8,128)(2,1)}, u32[]{:S(2)}) copy-start(bf16[1,896,512]{2,1,0:T(8,128)(2,1)} %param.10) | copy-start | bytes 2752516
  161.4 245.1 %all-reduce.6.cloned.1.call-start = ((), (), s32[]{:S(2)}) async-start(), calls=%async_computation.7 | async-start | bytes 3145728 | tf_op jit(solution)/shard_map/psum | solution.py:53
  203.1 296.3 %all-reduce.4.cloned.1.call-start = ((), (), s32[]{:S(2)}) async-start(), calls=%async_computation.4 | async-start | bytes 3145728 | tf_op jit(solution)/shard_map/psum | solution.py:54
  243.2 390.0 %all-reduce.8.cloned.1.call-start = ((), (), s32[]{:S(2)}) async-start(), calls=%async_computation.8 | async-start | bytes 5505024 | tf_op jit(solution)/shard_map/psum | solution.py:63
Sparse Core Ops, SparseCore 0:
  14.0 72.5 reduce-scatter.4
  89.1 70.4 reduce-scatter.2
  162.1 37.2 all-gather.4
  201.6 37.4 all-gather.2
  242.2 164.1 all-reduce.5
  409.5 89.8 all-reduce.3
  505.6 127.5 all-reduce.7
where the time goes:
time: 653 us; the launch traced here: 652 us
  waiting for transfers between devices  590 us (90%)
  matrix products  29.8 us (5%)
  between operations  14.8 us (2%)
  other arithmetic  9.67 us (1%)
  local copies, waits for them, and re-layouts  7.1 us (1%)
    psum x1, waiting for transfers between devices, body(): teacher = lax.psum(teacher_part, ('group', 'mp'))  163 us
    psum x1, waiting for transfers between devices, body(): hidden_full = lax.psum(hidden_part, 'dp')  124 us
    psum x1, waiting for transfers between devices, body(): student = lax.psum(student_part, 'mp')  93 us
    reduce_scatter x1, waiting for transfers between devices, body(): lax.psum_scatter(variant_term, 'dp', scatter_dimension=0, tiled=True)  71.3 us
    reduce_scatter x1, waiting for transfers between devices, body(): lax.psum_scatter(parent_term, 'dp', scatter_dimension=0, tiled=True)  66 us
    all_gather x1, waiting for transfers between devices, body(): lax.all_gather(parent_hidden, 'dp', axis=0, tiled=True)  38 us
    all_gather x1, waiting for transfers between devices, body(): lax.all_gather(variant_pre, 'dp', axis=0, tiled=True)  35.3 us
  transfers between devices with their start and end apart: 7, of which 7 were waited for; matrix products, arithmetic and copies ran while one was open for 3% of the time, Pallas kernels for 0%

commit v1 on v0

--- a/solution.py
+++ b/solution.py
@@ -3,6 +3,7 @@
 import jax.numpy as jnp
 from jax import lax
 from jax.sharding import PartitionSpec as P
+from jax.lax import all_to_all, axis_size
 
 
 def gated_values(pre_act, unit_mask):
@@ -43,8 +44,15 @@
     parent_pre = parent_rows.astype(jnp.bfloat16)
     variant_pre = variant_rows.astype(jnp.bfloat16)
     parent_hidden = gated_values(parent_pre, 1.0)
+
+    def measure_panel(s0, axis_id="dp"):
+        upper = axis_size(axis_id)
+        piece_next = jnp.stack(upper * [s0], axis=0)
+        frame_out = all_to_all(piece_next, axis_id, 0, 0)
+        return jnp.concatenate(frame_out, axis=0)
+
     parent_all, variant_all = (
-        lax.all_gather(parent_hidden, "dp", axis=0, tiled=True),
+        measure_panel(parent_hidden),
         lax.all_gather(variant_pre, "dp", axis=0, tiled=True),
     )
     variant_hidden = gated_values(variant_all, unit_mask)

time: 653 us -> 620 us (0.949)
  waiting for transfers between devices: 590 us -> 530 us
  blocking collectives: 0 us -> 29.1 us
    all_gather x1 -> x0, waiting for transfers between devices: 38 us -> none  [body(): lax.all_gather(parent_hidden, 'dp', axis=0, tiled=True)]
    all_to_all x0 -> x1, blocking collectives: none -> 29.1 us  [measure_panel(): frame_out = all_to_all(piece_next, axis_id, 0, 0)]
    all_gather x1, waiting for transfers between devices: 35.3 us -> 13.1 us  [body(): lax.all_gather(variant_pre, 'dp', axis=0, tiled=True)]
  transfers between devices with their start and end apart: 7 -> 6, of which waited for: 7 -> 6; matrix products, arithmetic and copies ran while one was open for 3% -> 3% of each run, Pallas kernels for 0% -> 0%
where the time goes in v1:
time: 620 us; the launch traced here: 619 us
  waiting for transfers between devices  530 us (85%)
  matrix products  29.4 us (5%)
  blocking collectives  29.1 us (5%)
  between operations  14.8 us (2%)
  other arithmetic  9.03 us (1%)
  local copies, waits for them, and re-layouts  7.2 us (1%)
    psum x1, waiting for transfers between devices, body(): teacher = lax.psum(teacher_part, ('group', 'mp'))  163 us
    psum x1, waiting for transfers between devices, body(): hidden_full = lax.psum(hidden_part, 'dp')  124 us
    psum x1, waiting for transfers between devices, body(): student = lax.psum(student_part, 'mp')  93 us
    reduce_scatter x1, waiting for transfers between devices, body(): lax.psum_scatter(parent_term, 'dp', scatter_dimension=0, tiled=True)  71.3 us
    reduce_scatter x1, waiting for transfers between devices, body(): lax.psum_scatter(variant_term, 'dp', scatter_dimension=0, tiled=True)  66 us
    all_to_all x1, blocking collectives, measure_panel(): frame_out = all_to_all(piece_next, axis_id, 0, 0)  29.1 us
    all_gather x1, waiting for transfers between devices, body(): lax.all_gather(variant_pre, 'dp', axis=0, tiled=True)  13.1 us
  transfers between devices with their start and end apart: 6, of which 6 were waited for; matrix products, arithmetic and copies ran while one was open for 3% of the time, Pallas kernels for 0%

profile of v1, /device:TPU:1, one launch (start us, length us, event | category | flops | bytes accessed | tf_op | source)
XLA Modules:
  0.0 619.5 jit_solution(10581348596636356272)
XLA Ops:
  7.2 0.0 copy-start
  7.2 0.0 reduce-scatter.3.cloned.1.call-start
  7.2 1.4 copy-done
  8.7 5.2 fusion.29
  13.9 0.0 copy-start.1
  13.9 0.0 reduce-scatter.3.cloned.1.call-update
  13.9 0.0 reduce-scatter.5.cloned.1.call-start
  13.9 1.1 copy-done.1
  15.0 5.5 fusion.45
  20.5 0.0 reduce-scatter.5.cloned.1.call-update
  20.5 0.0 all-gather.2.cloned.1.call-start
  20.6 66.0 %reduce-scatter.3.cloned.1.call-done = f32[48,2,896]{2,0,1:T(8,128)} async-done(((f32[768,2,896]{2,0,1:T(8,128)}), f32[48,2,896]{2,0,1:T(8,128)}) %reduce-scatter.3.cloned.1.call-update) | async-done | bytes 344080 | tf_op jit(solution)/shard_map/reduce_scatter | solution.py:42
  86.6 1.7 convert_element_type.66
  88.2 0.0 all-gather.2.cloned.1.call-update
  88.3 0.0 all-reduce.6.cloned.1.call-start
  88.3 71.3 %reduce-scatter.5.cloned.1.call-done = f32[48,2,896]{2,0,1:T(8,128)} async-done(((f32[768,2,896]{2,0,1:T(8,128)}), f32[48,2,896]{2,0,1:T(8,128)}) %reduce-scatter.5.cloned.1.call-update) | async-done | bytes 344080 | tf_op jit(solution)/shard_map/reduce_scatter | solution.py:41
  159.6 1.0 convert_element_type.72
  160.7 0.1 fusion.52
  160.7 0.1 stack.11
  160.8 29.1 %all_to_all.5 = bf16[16,48,896]{2,1,0:T(8,128)(2,1)S(1)} all-to-all(bf16[16,48,896]{2,1,0:T(8,128)(2,1)S(1)} %stack.11), channel_id=1, replica_groups=mesh['group'=4,'dp'=16,'mp'=4] {'dp'}, dimensions={0} | all-to-all | bytes 2752512 | tf_op jit(solution)/shard_map/all_to_all | solution.py:51
  189.9 0.0 copy-start.2
  190.0 3.4 fusion.57
  193.3 0.0 all-reduce.6.cloned.1.call-update
  193.4 0.0 all-reduce.4.cloned.1.call-start
  194.1 13.1 %all-gather.2.cloned.1.call-done = bf16[768,2,896]{2,0,1:T(8,128)(2,1)} async-done(((bf16[48,2,896]{2,0,1:T(8,128)(2,1)}), bf16[768,2,896]{2,0,1:T(8,128)(2,1)}) %all-gather.2.cloned.1.call-update) | async-done | bytes 2752528 | tf_op jit(solution)/shard_map/all_gather | solution.py:56
  207.2 0.0 copy-done.2
  207.2 4.0 fusion.31
  211.2 0.0 all-reduce.4.cloned.1.call-update
  211.2 0.0 all-reduce.8.cloned.1.call-start
  211.3 162.5 %all-reduce.6.cloned.1.call-done = f32[768,512]{1,0:T(8,128)} async-done(((f32[768,512]{1,0:T(8,128)}), f32[768,512]{1,0:T(8,128)}) %all-reduce.6.cloned.1.call-update) | async-done | bytes 1572880 | tf_op jit(solution)/shard_map/psum | solution.py:61
  373.8 93.0 %all-reduce.4.cloned.1.call-done = f32[768,512]{1,0:T(8,128)} async-done(((f32[768,512]{1,0:T(8,128)}), f32[768,512]{1,0:T(8,128)}) %all-reduce.4.cloned.1.call-update) | async-done | bytes 1572880 | tf_op jit(solution)/shard_map/psum | solution.py:62
  466.8 2.3 multiply_convert_fusion
  469.1 3.7 fusion.39
  472.8 0.0 all-reduce.8.cloned.1.call-update
  472.9 4.1 convolution_bitcast_fusion
  477.0 123.6 %all-reduce.8.cloned.1.call-done = f32[768,896]{1,0:T(8,128)} async-done(((f32[768,896]{1,0:T(8,128)}), f32[768,896]{1,0:T(8,128)}) %all-reduce.8.cloned.1.call-update) | async-done | bytes 2752528 | tf_op jit(solution)/shard_map/psum | solution.py:71
  600.6 4.0 fusion.36
  604.6 3.4 fusion.26
  608.1 4.6 copy.9
  (1 shorter events, 0.0 us)
Async XLA Ops:
  7.2 1.5 copy-start
  7.2 79.4 %reduce-scatter.3.cloned.1.call-start = ((), (), s32[]{:S(2)}) async-start(), calls=%async_computation.3 | async-start | bytes 5849088 | tf_op jit(solution)/shard_map/reduce_scatter | solution.py:42
  13.9 1.1 copy-start.1
  13.9 145.8 %reduce-scatter.5.cloned.1.call-start = ((), (), s32[]{:S(2)}) async-start(), calls=%async_computation.6 | async-start | bytes 5849088 | tf_op jit(solution)/shard_map/reduce_scatter | solution.py:41
  20.5 186.7 %all-gather.2.cloned.1.call-start = ((), (), s32[]{:S(2)}) async-start(), calls=%async_computation.4 | async-start | bytes 2924544 | tf_op jit(solution)/shard_map/all_gather | solution.py:56
  88.3 285.6 %all-reduce.6.cloned.1.call-start = ((), (), s32[]{:S(2)}) async-start(), calls=%async_computation.7 | async-start | bytes 3145728 | tf_op jit(solution)/shard_map/psum | solution.py:61
  189.9 17.3 %copy-start.2 = (bf16[1,896,512]{2,1,0:T(8,128)(2,1)S(1)}, bf16[1,896,512]{2,1,0:T(8,128)(2,1)}, u32[]{:S(2)}) copy-start(bf16[1,896,512]{2,1,0:T(8,128)(2,1)} %param.10) | copy-start | bytes 2752516
  193.4 273.5 %all-reduce.4.cloned.1.call-start = ((), (), s32[]{:S(2)}) async-start(), calls=%async_computation.5 | async-start | bytes 3145728 | tf_op jit(solution)/shard_map/psum | solution.py:62
  211.2 389.4 %all-reduce.8.cloned.1.call-start = ((), (), s32[]{:S(2)}) async-start(), calls=%async_computation.8 | async-start | bytes 5505024 | tf_op jit(solution)/shard_map/psum | solution.py:71
Sparse Core Ops, SparseCore 0:
  14.0 72.5 reduce-scatter.2
  89.1 70.4 reduce-scatter.4
  162.0 45.1 all-gather.1
  210.3 163.5 all-reduce.5
  376.9 89.8 all-reduce.3
  473.0 127.5 all-reduce.7
